TPU v7x, 32 devices: a whole 2x2x4 slice. The times are simulated.
32 devices in a mesh: aa: 8 (over z, x), ba: 4 (over y, core).
Axes of the slice: x: 2, y: 2, z: 4, core: 2. Of those that a mesh axis runs over, the one named last changes fastest.
Arguments:
- grid_features: bfloat16 [128, 128, 256, 128], P('aa', 'ba'), may hold values from -6 to 6
- weight_real: bfloat16 [32, 32, 16, 128, 128], P('ba', None, 'aa'), may hold values from -6 to 6
- weight_imag: bfloat16 [32, 32, 16, 128, 128], P('ba', None, 'aa'), may hold values from -6 to 6
- mode_keep: int32 [32, 16], P('ba', 'aa'), may hold values from 1 to 16, as said below
- local_weight: bfloat16 [128, 128], replicated, may hold values from -0.5 to 0.5
- local_bias: bfloat16 [128], replicated, may hold values from -3 to 3
Outputs:
- layer_output: bfloat16 [128, 128, 256, 128], P('aa', 'ba')
Inputs may be any that keep to these rules, and one draw needn't show every extreme that they name: mode_keep[i, k] counts the retained levels of the second frequency on the line of the i-th retained first frequency and the k-th third frequency.
All inputs are finite; a program needn't handle non-finite values.
Results may differ from a plain program's by a relative error of at most 0.012.
Values may be sent and summed in bfloat16 or wider, within the bound.
A program may use at most 256 MiB of HBM per device.

v0:
```python
import functools
import math

import jax
import jax.numpy as jnp
from jax import lax
from jax.experimental import pallas as pl
from jax.experimental.pallas import tpu as pltpu
from jax.sharding import PartitionSpec as P

CHUNKS = 2
BF = jnp.bfloat16
F32 = jnp.float32


def kept_modes(length, number, positions):
    return jnp.where(positions < number // 2, positions, positions + (length - number))


def phase_tables(length, places, mode_list):
    phase_steps = places[:, None] * mode_list[None, :] % length
    angles = phase_steps.astype(F32) * (2.0 * math.pi / length)
    return jnp.cos(angles), jnp.sin(angles)


def forward_table(length, places, modes):
    c, s = phase_tables(length, places, modes)
    return jnp.stack([jnp.stack([c, -s], 1), jnp.stack([s, c], 1)], 0).astype(BF)


def inverse_table(length, places, modes):
    c, s = phase_tables(length, places, modes)
    c, s = c.T, s.T
    return jnp.stack([jnp.stack([c, s], 1), jnp.stack([-s, c], 1)], 0).astype(BF)


def depth_body(table_ref, x_ref, out_ref):
    rows = x_ref.shape[1]
    chans = x_ref.shape[3]
    for j in range(rows // 2):
        pair = jnp.concatenate([x_ref[0, 2 * j], x_ref[0, 2 * j + 1]], axis=1)
        res = jnp.dot(table_ref[...], pair, preferred_element_type=F32).astype(BF)
        out_ref[0, 2 * j] = res[:, :chans]
        out_ref[0, 2 * j + 1] = res[:, chans:]


def depth_forward(grid_features, table, first, count):
    _, rows, depth, chans = grid_features.shape
    modes = table.shape[0]
    return pl.pallas_call(
        depth_body,
        grid=(count,),
        in_specs=[
            pl.BlockSpec((modes, depth), lambda i: (0, 0)),
            pl.BlockSpec((1, rows, depth, chans), lambda i: (i + first, 0, 0, 0)),
        ],
        out_specs=pl.BlockSpec((1, rows, modes, chans), lambda i: (i, 0, 0, 0)),
        out_shape=jax.ShapeDtypeStruct((count, rows, modes, chans), BF),
        compiler_params=pltpu.CompilerParams(vmem_limit_bytes=24 << 20),
        cost_estimate=pl.CostEstimate(
            flops=2 * count * rows * depth * chans * modes * 16,
            bytes_accessed=2 * count * rows * depth * chans,
            transcendentals=0,
        ),
    )(table, grid_features)


def final_body(table_ref, w_ref, bias_ref, x_ref, back_ref, *rest):
    out_ref = rest[-1]
    bias = bias_ref[...]
    c1 = math.sqrt(2.0 / math.pi)

    for j in range(x_ref.shape[1]):
        val = jnp.dot(x_ref[0, j], w_ref[...], preferred_element_type=F32)
        val = val + jnp.dot(table_ref[...], back_ref[0, j], preferred_element_type=F32)
        val = val + bias
        inner = val * (c1 + (c1 * 0.044715) * (val * val))
        half = 0.5 * val
        out_ref[0, j] = (half + half * jnp.tanh(inner)).astype(BF)


def finish(grid_features, back, table, weight, bias, first, so_far):
    total, rows, depth, chans = grid_features.shape
    count, _, modes, _ = back.shape
    block = 8
    while rows % block:
        block //= 2
    big = pl.BlockSpec((1, block, depth, chans), lambda i, j: (i + first, j, 0, 0))
    in_specs = [
        pl.BlockSpec((depth, modes), lambda i, j: (0, 0)),
        pl.BlockSpec((chans, chans), lambda i, j: (0, 0)),
        pl.BlockSpec((1, chans), lambda i, j: (0, 0)),
        big,
        pl.BlockSpec((1, block, modes, chans), lambda i, j: (i, j, 0, 0)),
    ]
    operands = [table, weight, bias, grid_features, back]
    aliases = {}
    if so_far is not None:
        in_specs.append(pl.BlockSpec(memory_space=pl.ANY))
        operands.append(so_far)
        aliases = {5: 0}
    return pl.pallas_call(
        final_body,
        grid=(count, rows // block),
        in_specs=in_specs,
        out_specs=big,
        out_shape=jax.ShapeDtypeStruct(grid_features.shape, BF),
        input_output_aliases=aliases,
        compiler_params=pltpu.CompilerParams(vmem_limit_bytes=24 << 20),
        cost_estimate=pl.CostEstimate(
            flops=2 * count * rows * depth * chans * (chans + modes) * 8,
            bytes_accessed=4 * count * rows * depth * chans,
            transcendentals=count * rows * depth * chans,
        ),
    )(*operands)


def per_device(
    n_aa, n_ba, grid_features, weight_real, weight_imag, mode_keep, local_weight, local_bias
):
    n_x, n_y, depth, chans = grid_features.shape
    kx_own, ky, kz_own = weight_real.shape[:3]
    nx, ny = n_x * n_aa, n_y * n_ba
    kx, kz, ky_own = kx_own * n_ba, kz_own * n_aa, ky // n_ba
    bits = n_ba.bit_length() - 1
    me = lax.axis_index("ba")

    c, s = phase_tables(depth, jnp.arange(depth), jnp.arange(kz))
    depth_fwd = jnp.concatenate([c, -s], axis=1).T.astype(BF)
    factor = jnp.where(jnp.arange(kz) == 0, 1.0, 2.0).astype(F32) / (nx * ny * depth)
    depth_inv = jnp.concatenate([c * factor, -s * factor], axis=1).astype(BF)

    order = jnp.arange(n_ba)
    block = jnp.zeros_like(order)
    for bit in range(bits):
        block = block + ((order >> (bits - 1 - bit)) & 1) * (1 << bit)
    block = block ^ me
    ky_pos = (block[:, None] * ky_own + jnp.arange(ky_own)[None, :]).reshape(-1)
    ky_modes = kept_modes(ny, ky, ky_pos)
    own_y = me * n_y + jnp.arange(n_y)
    y_fwd = forward_table(ny, own_y, ky_modes)
    y_inv = inverse_table(ny, own_y, ky_modes)
    x_modes = kept_modes(nx, kx, jnp.arange(kx))
    x_fwd = forward_table(nx, jnp.arange(nx), x_modes)
    x_inv = inverse_table(nx, jnp.arange(nx), x_modes)

    def swap(value, bit):
        return lax.ppermute(value, "ba", [(i, i ^ (1 << bit)) for i in range(n_ba)])

    per = n_x // CHUNKS
    landed = []
    for ch in range(CHUNKS):
        coeffs = depth_forward(grid_features, depth_fwd, ch * per, per)
        coeffs = coeffs.reshape(per, n_y, 2, kz, chans)
        part = jnp.einsum("xypkc,pyrq->qrxkc", coeffs, y_fwd, preferred_element_type=F32)
        for bit in range(bits):
            half = part.shape[0] // 2
            got = swap(part[half:].astype(BF), bit)
            part = part[:half] + got.astype(F32)
        part = part.astype(BF).reshape(ky_own, 2, per, n_aa, kz_own, chans)
        part = jnp.transpose(part, (3, 2, 0, 1, 4, 5))
        landed.append(lax.all_to_all(part, "aa", 0, 0, tiled=True))
    field = jnp.stack(landed, 1).reshape(nx, ky_own, 2, kz_own, chans)
    spec = jnp.einsum("xqpkc,pxrm->mrqkc", field, x_fwd, preferred_element_type=F32).astype(BF)
    spec = spec.reshape(n_ba, kx_own, 2, ky_own, kz_own, chans)
    spec = lax.all_to_all(spec, "ba", 0, 0, tiled=True)
    spec = jnp.transpose(spec, (1, 0, 3, 4, 2, 5)).reshape(kx_own, ky, kz_own, 2, chans)

    pattern = "abcmd,abcde->abcme"
    by_real = jnp.einsum(pattern, spec, weight_real, preferred_element_type=F32)
    by_imag = jnp.einsum(pattern, spec, weight_imag, preferred_element_type=F32)
    out_real = by_real[..., 0, :] - by_imag[..., 1, :]
    out_imag = by_imag[..., 0, :] + by_real[..., 1, :]
    positions = jnp.arange(ky)
    levels = jnp.where(positions < ky // 2, positions, ky - 1 - positions)
    keep = (levels[None, :, None] < mode_keep[:, None, :]).astype(F32)[..., None]
    mixed = jnp.stack([out_real * keep, out_imag * keep], 0).astype(BF)
    mixed = mixed.reshape(2, kx_own, n_ba, ky_own, kz_own, chans)
    mixed = jnp.transpose(mixed, (2, 1, 0, 3, 4, 5))
    mixed = lax.all_to_all(mixed, "ba", 0, 0, tiled=True)
    mixed = mixed.reshape(kx, 2, ky_own, kz_own, chans)
    back = jnp.einsum("mpqkc,pmrx->xqrkc", mixed, x_inv, preferred_element_type=F32).astype(BF)
    back = back.reshape(n_aa, CHUNKS, per, ky_own, 2, kz_own, chans)

    bias = local_bias.astype(F32).reshape(1, chans)
    fields = []
    for ch in range(CHUNKS):
        piece = lax.all_to_all(back[:, ch], "aa", 0, 0, tiled=True)
        piece = jnp.transpose(piece, (2, 3, 1, 0, 4, 5))
        piece = piece.reshape(ky_own, 2, per, kz, chans)
        for bit in reversed(range(bits)):
            piece = jnp.concatenate([piece, swap(piece, bit)], axis=0)
        field = jnp.einsum("qpxkc,pqry->xyrkc", piece, y_inv, preferred_element_type=F32)
        fields.append(field.astype(BF).reshape(per, n_y, 2 * kz, chans))
    result = None
    for ch in range(CHUNKS):
        result = finish(
            grid_features, fields[ch], depth_inv, local_weight, bias, ch * per, result
        )
    return result


def solution(mesh):
    in_specs = (
        P("aa", "ba", None, None),
        P("ba", None, "aa", None, None),
        P("ba", None, "aa", None, None),
        P("ba", "aa"),
        P(),
        P(),
    )
    out_specs = P("aa", "ba", None, None)
    body = functools.partial(per_device, mesh.shape["aa"], mesh.shape["ba"])
    return jax.shard_map(body, mesh=mesh, in_specs=in_specs, out_specs=out_specs, check_vma=False)
```

profile of v0, /device:TPU:27, one launch (start us, length us, event | category | flops | bytes accessed | tf_op | source)
XLA Modules:
  0.0 233.3 jit_solution(5766569202670733205)
XLA Ops:
  0.5 9.3 %shard_map.64 = bf16[8,32,32,128]{3,2,1,0:T(8,128)(2,1)S(1)} custom-call(bf16[32,256]{1,0:T(8,128)(2,1)S(1)} %maximum_bitcast_fusion.25.table_ref, bf16[16,32,256,128]{3,2,1,0:T(8,128)(2,1)} %x_ref.7), custom_call_target="tpu_custom_call" | custom-call | flops 8589934592 | bytes 16777216 | tf_op jit(solution)/shard_map/pallas_call | solution.py:50
  11.7 9.3 %shard_map.65 = bf16[8,32,32,128]{3,2,1,0:T(8,128)(2,1)S(1)} custom-call(bf16[32,256]{1,0:T(8,128)(2,1)S(1)} %maximum_bitcast_fusion.25.table_ref, bf16[16,32,256,128]{3,2,1,0:T(8,128)(2,1)} %x_ref.7), custom_call_target="tpu_custom_call" | custom-call | flops 8589934592 | bytes 16777216 | tf_op jit(solution)/shard_map/pallas_call | solution.py:50
  21.8 2.0 copy-done.1
  24.6 1.3 collective-permute-start.1
  25.9 11.8 %collective-permute-done.1 = bf16[8,2,8,16,128]{4,0,3,2,1:T(8,128)(2,1)S(1)} collective-permute-done((bf16[8,2,8,16,128]{4,0,3,2,1:T(8,128)(2,1)S(1)}, bf16[8,2,8,16,128]{4,0,3,2,1:T(8,128)(2,1)S(1)}, u32[]{:S(2)}, u32[]{:S(2)}) %collective-permute-start.1) | collective-permute-done | bytes 524320 | tf_op jit(solution)/shard_map/ppermute | solution.py:148
  37.8 0.9 copy.149
  38.7 5.4 %all-to-all-start = ((bf16[8,8,8,2,2,128]{5,2,4,1,3,0:T(8,128)(2,1)}), bf16[8,8,8,2,2,128]{5,2,4,1,3,0:T(8,128)(2,1)S(1)}, u32[]{:S(2)}, u32[]{:S(2)}) async-start(bf16[8,8,8,2,2,128]{5,2,4,1,3,0:T(8,128)(2,1)} %bitcast.149), calls=%async_computation | async-start | bytes 1048576 | tf_op jit(solution)/shard_map/all_to_all | solution.py:162
  44.1 1.9 slice_add_fusion
  46.1 1.3 collective-permute-start.3
  47.4 10.3 %collective-permute-done.3 = bf16[8,2,8,16,128]{4,0,3,2,1:T(8,128)(2,1)S(1)} collective-permute-done((bf16[8,2,8,16,128]{4,0,3,2,1:T(8,128)(2,1)S(1)}, bf16[8,2,8,16,128]{4,0,3,2,1:T(8,128)(2,1)S(1)}, u32[]{:S(2)}, u32[]{:S(2)}) %collective-permute-start.3) | collective-permute-done | bytes 524320 | tf_op jit(solution)/shard_map/ppermute | solution.py:148
  58.8 5.4 %all-to-all-start.1 = ((bf16[8,8,8,2,2,128]{5,2,4,1,3,0:T(8,128)(2,1)}), bf16[8,8,8,2,2,128]{5,2,4,1,3,0:T(8,128)(2,1)S(1)}, u32[]{:S(2)}, u32[]{:S(2)}) async-start(bf16[8,8,8,2,2,128]{5,2,4,1,3,0:T(8,128)(2,1)} %bitcast.148), calls=%async_computation.1 | async-start | bytes 1048576 | tf_op jit(solution)/shard_map/all_to_all | solution.py:162
  64.5 11.4 %all-to-all-done.1 = bf16[8,8,8,2,2,128]{5,2,4,1,3,0:T(8,128)(2,1)S(1)} async-done(((bf16[8,8,8,2,2,128]{5,2,4,1,3,0:T(8,128)(2,1)}), bf16[8,8,8,2,2,128]{5,2,4,1,3,0:T(8,128)(2,1)S(1)}, u32[]{:S(2)}, u32[]{:S(2)}) %all-to-all-start.1) | async-done | bytes 524320 | tf_op jit(solution)/shard_map/all_to_all | solution.py:162
  77.3 5.1 %all-to-all-start.2 = ((bf16[4,8,2,8,2,128]{5,1,4,3,2,0:T(8,128)(2,1)}), bf16[4,8,2,8,2,128]{5,1,4,3,2,0:T(8,128)(2,1)S(1)}, u32[]{:S(2)}, u32[]{:S(2)}) async-start(bf16[4,8,2,8,2,128]{5,1,4,3,2,0:T(8,128)(2,1)} %copy.80), calls=%async_computation.2 | async-start | bytes 524288 | tf_op jit(solution)/shard_map/all_to_all | solution.py:166
  82.5 5.0 %all-to-all-done.2 = bf16[4,8,2,8,2,128]{5,1,4,3,2,0:T(8,128)(2,1)S(1)} async-done(((bf16[4,8,2,8,2,128]{5,1,4,3,2,0:T(8,128)(2,1)}), bf16[4,8,2,8,2,128]{5,1,4,3,2,0:T(8,128)(2,1)S(1)}, u32[]{:S(2)}, u32[]{:S(2)}) %all-to-all-start.2) | async-done | bytes 262176 | tf_op jit(solution)/shard_map/all_to_all | solution.py:166
  87.7 8.0 %fusion.78 = f32[8,32,2,2,128]{4,3,2,1,0:T(2,128)S(1)} fusion(bf16[8,32,2,2,128]{4,3,2,1,0:T(2,128)(2,1)S(1)} %bitcast.156, bf16[8,32,2,128,128]{4,3,2,1,0:T(8,128)(2,1)} %param.8), kind=kOutput, calls=%fused_computation.160 | convolution fusion | flops 33554432 | bytes 17563648 | tf_op jit(solution)/shard_map/abcmd,abcde->abcme/dot_general | solution.py:171
  95.8 8.0 %fusion.77 = f32[8,32,2,2,128]{4,3,2,1,0:T(2,128)S(1)} fusion(bf16[8,32,2,2,128]{4,3,2,1,0:T(2,128)(2,1)S(1)} %bitcast.157, bf16[8,32,2,128,128]{4,3,2,1,0:T(8,128)(2,1)} %param.7), kind=kOutput, calls=%fused_computation.159 | convolution fusion | flops 33554432 | bytes 17563648 | tf_op jit(solution)/shard_map/abcmd,abcde->abcme/dot_general | solution.py:170
  104.6 0.9 copy.87
  105.5 4.3 %all-to-all-start.3 = ((bf16[4,8,2,8,2,128]{5,4,3,1,2,0:T(2,128)(2,1)}), bf16[4,8,2,8,2,128]{5,4,3,1,2,0:T(2,128)(2,1)S(1)}, u32[]{:S(2)}, u32[]{:S(2)}) async-start(bf16[4,8,2,8,2,128]{5,4,3,1,2,0:T(2,128)(2,1)} %copy.87), calls=%async_computation.3 | async-start | bytes 524288 | tf_op jit(solution)/shard_map/all_to_all | solution.py:180
  110.0 4.9 %all-to-all-done.3 = bf16[4,8,2,8,2,128]{5,4,3,1,2,0:T(2,128)(2,1)S(1)} async-done(((bf16[4,8,2,8,2,128]{5,4,3,1,2,0:T(2,128)(2,1)}), bf16[4,8,2,8,2,128]{5,4,3,1,2,0:T(2,128)(2,1)S(1)}, u32[]{:S(2)}, u32[]{:S(2)}) %all-to-all-start.3) | async-done | bytes 262176 | tf_op jit(solution)/shard_map/all_to_all | solution.py:180
  115.6 0.9 copy.147
  116.6 5.5 %all-to-all-start.4 = ((bf16[8,8,8,2,2,128]{5,1,4,2,3,0:T(8,128)(2,1)}), bf16[8,8,8,2,2,128]{5,1,4,2,3,0:T(8,128)(2,1)S(1)}, u32[]{:S(2)}, u32[]{:S(2)}) async-start(bf16[8,8,8,2,2,128]{5,1,4,2,3,0:T(8,128)(2,1)} %bitcast.147), calls=%async_computation.4 | async-start | bytes 1048576 | tf_op jit(solution)/shard_map/all_to_all | solution.py:188
  122.1 0.9 copy.146
  123.0 11.7 %all-to-all-done.4 = bf16[8,8,8,2,2,128]{5,1,4,2,3,0:T(8,128)(2,1)S(1)} async-done(((bf16[8,8,8,2,2,128]{5,1,4,2,3,0:T(8,128)(2,1)}), bf16[8,8,8,2,2,128]{5,1,4,2,3,0:T(8,128)(2,1)S(1)}, u32[]{:S(2)}, u32[]{:S(2)}) %all-to-all-start.4) | async-done | bytes 524320 | tf_op jit(solution)/shard_map/all_to_all | solution.py:188
  134.7 5.4 %all-to-all-start.5 = ((bf16[8,8,8,2,2,128]{5,1,4,2,3,0:T(8,128)(2,1)}), bf16[8,8,8,2,2,128]{5,1,4,2,3,0:T(8,128)(2,1)S(1)}, u32[]{:S(2)}, u32[]{:S(2)}) async-start(bf16[8,8,8,2,2,128]{5,1,4,2,3,0:T(8,128)(2,1)} %bitcast.146), calls=%async_computation.5 | async-start | bytes 1048576 | tf_op jit(solution)/shard_map/all_to_all | solution.py:188
  141.0 12.0 %all-to-all-done.5 = bf16[8,8,8,2,2,128]{5,1,4,2,3,0:T(8,128)(2,1)S(1)} async-done(((bf16[8,8,8,2,2,128]{5,1,4,2,3,0:T(8,128)(2,1)}), bf16[8,8,8,2,2,128]{5,1,4,2,3,0:T(8,128)(2,1)S(1)}, u32[]{:S(2)}, u32[]{:S(2)}) %all-to-all-start.5) | async-done | bytes 524320 | tf_op jit(solution)/shard_map/all_to_all | solution.py:188
  153.9 1.2 pad_maximum_fusion.1
  155.8 10.4 %collective-permute-done.6 = bf16[8,2,8,16,128]{4,0,1,3,2:T(8,128)(2,1)S(1)} collective-permute-done((bf16[8,2,8,16,128]{4,0,1,3,2:T(8,128)(2,1)S(1)}, bf16[8,2,8,16,128]{4,0,1,3,2:T(8,128)(2,1)S(1)}, u32[]{:S(2)}, u32[]{:S(2)}) %collective-permute-start.6) | collective-permute-done | bytes 524320 | tf_op jit(solution)/shard_map/ppermute | solution.py:148
  166.4 1.4 collective-permute-start.7
  168.1 2.0 fusion.12
  170.9 2.0 fusion.13
  173.7 29.8 %shard_map.66.rest_0_ = bf16[16,32,256,128]{3,2,1,0:T(8,128)(2,1)} custom-call(bf16[256,32]{1,0:T(8,128)(2,1)S(1)} %copy.98.table_ref, bf16[128,128]{1,0:T(8,128)(2,1)S(1)} %copy-done, f32[1,128]{1,0:T(1,128)S(1)} %bitcast_convert_fusion.3.bias_ref, bf16[16,32,256,128]{3,2,1,0:T(8,128)(2,1)} %x_ref.7, bf16[8,32,32,128]{3,2,1,0:T(8,128)(2,1)S(1)} %bitcast.153), custom_call_target="tpu_custom_call" | custom-call | flops 21474836480 | bytes 33554432 | tf_op jit(solution)/shard_map/pallas_call | solution.py:102
  203.5 29.8 %shard_map.67 = bf16[16,32,256,128]{3,2,1,0:T(8,128)(2,1)} custom-call(bf16[256,32]{1,0:T(8,128)(2,1)S(1)} %copy.98.table_ref, bf16[128,128]{1,0:T(8,128)(2,1)S(1)} %copy-done, f32[1,128]{1,0:T(1,128)S(1)} %bitcast_convert_fusion.3.bias_ref, bf16[16,32,256,128]{3,2,1,0:T(8,128)(2,1)} %x_ref.7, ...), custom_call_target="tpu_custom_call", output_to_operand_aliasing={{}: (5, {})} | custom-call | flops 21474836480 | bytes 33554432 | tf_op jit(solution)/shard_map/pallas_call | solution.py:102
  (65 shorter events, 13.4 us)
Async XLA Ops:
  10.9 13.3 %collective-permute-start = (bf16[16,2,8,16,128]{4,0,3,2,1:T(8,128)(2,1)S(1)}, bf16[16,2,8,16,128]{4,0,3,2,1:T(8,128)(2,1)S(1)}, u32[]{:S(2)}, u32[]{:S(2)}) collective-permute-start(bf16[16,2,8,16,128]{4,0,3,2,1:T(8,128)(2,1)S(1)} %slice.91), channel_id=1, source_target_pairs={{0,1},{1,0},{2,3},{3,2},{4,5},{5,4},{6,7},{7,6},{8,9},{9,8},{10,11... | collective-permute-start | bytes 3145736 | tf_op jit(solution)/shard_map/ppermute | solution.py:148
  21.8 2.0 copy-start.1
  24.1 20.0 %collective-permute-start.2 = (bf16[16,2,8,16,128]{4,0,3,2,1:T(8,128)(2,1)S(1)}, bf16[16,2,8,16,128]{4,0,3,2,1:T(8,128)(2,1)S(1)}, u32[]{:S(2)}, u32[]{:S(2)}) collective-permute-start(bf16[16,2,8,16,128]{4,0,3,2,1:T(8,128)(2,1)S(1)} %slice.90), channel_id=1, source_target_pairs={{0,1},{1,0},{2,3},{3,2},{4,5},{5,4},{6,7},{7,6},{8,9},{9,8},{10,11... | collective-permute-start | bytes 3145736 | tf_op jit(solution)/shard_map/ppermute | solution.py:148
  24.6 13.1 %collective-permute-start.1 = (bf16[8,2,8,16,128]{4,0,3,2,1:T(8,128)(2,1)S(1)}, bf16[8,2,8,16,128]{4,0,3,2,1:T(8,128)(2,1)S(1)}, u32[]{:S(2)}, u32[]{:S(2)}) collective-permute-start(bf16[8,2,8,16,128]{4,0,3,2,1:T(8,128)(2,1)S(1)} %slice.93), channel_id=1, source_target_pairs={{0,2},{1,3},{2,0},{3,1},{4,6},{5,7},{6,4},{7,5},{8,10},{9,11},{10,... | collective-permute-start | bytes 1572872 | tf_op jit(solution)/shard_map/ppermute | solution.py:148
  38.7 20.1 %all-to-all-start = ((bf16[8,8,8,2,2,128]{5,2,4,1,3,0:T(8,128)(2,1)}), bf16[8,8,8,2,2,128]{5,2,4,1,3,0:T(8,128)(2,1)S(1)}, u32[]{:S(2)}, u32[]{:S(2)}) async-start(bf16[8,8,8,2,2,128]{5,2,4,1,3,0:T(8,128)(2,1)} %bitcast.149), calls=%async_computation | async-start | bytes 1048576 | tf_op jit(solution)/shard_map/all_to_all | solution.py:162
  46.1 18.1 %copy-start.2 = (s32[8,2]{0,1:T(2,128)S(1)}, s32[8,2]{0,1:T(2,128)}, u32[]{:S(2)}) copy-start(s32[8,2]{0,1:T(2,128)} %param.9) | copy-start | bytes 196
  46.1 11.6 %collective-permute-start.3 = (bf16[8,2,8,16,128]{4,0,3,2,1:T(8,128)(2,1)S(1)}, bf16[8,2,8,16,128]{4,0,3,2,1:T(8,128)(2,1)S(1)}, u32[]{:S(2)}, u32[]{:S(2)}) collective-permute-start(bf16[8,2,8,16,128]{4,0,3,2,1:T(8,128)(2,1)S(1)} %slice.92), channel_id=1, source_target_pairs={{0,2},{1,3},{2,0},{3,1},{4,6},{5,7},{6,4},{7,5},{8,10},{9,11},{10,... | collective-permute-start | bytes 1572872 | tf_op jit(solution)/shard_map/ppermute | solution.py:148
  58.8 17.1 %all-to-all-start.1 = ((bf16[8,8,8,2,2,128]{5,2,4,1,3,0:T(8,128)(2,1)}), bf16[8,8,8,2,2,128]{5,2,4,1,3,0:T(8,128)(2,1)S(1)}, u32[]{:S(2)}, u32[]{:S(2)}) async-start(bf16[8,8,8,2,2,128]{5,2,4,1,3,0:T(8,128)(2,1)} %bitcast.148), calls=%async_computation.1 | async-start | bytes 1048576 | tf_op jit(solution)/shard_map/all_to_all | solution.py:162
  77.3 10.2 %all-to-all-start.2 = ((bf16[4,8,2,8,2,128]{5,1,4,3,2,0:T(8,128)(2,1)}), bf16[4,8,2,8,2,128]{5,1,4,3,2,0:T(8,128)(2,1)S(1)}, u32[]{:S(2)}, u32[]{:S(2)}) async-start(bf16[4,8,2,8,2,128]{5,1,4,3,2,0:T(8,128)(2,1)} %copy.80), calls=%async_computation.2 | async-start | bytes 524288 | tf_op jit(solution)/shard_map/all_to_all | solution.py:166
  105.5 9.4 %all-to-all-start.3 = ((bf16[4,8,2,8,2,128]{5,4,3,1,2,0:T(2,128)(2,1)}), bf16[4,8,2,8,2,128]{5,4,3,1,2,0:T(2,128)(2,1)S(1)}, u32[]{:S(2)}, u32[]{:S(2)}) async-start(bf16[4,8,2,8,2,128]{5,4,3,1,2,0:T(2,128)(2,1)} %copy.87), calls=%async_computation.3 | async-start | bytes 524288 | tf_op jit(solution)/shard_map/all_to_all | solution.py:180
  116.6 18.1 %all-to-all-start.4 = ((bf16[8,8,8,2,2,128]{5,1,4,2,3,0:T(8,128)(2,1)}), bf16[8,8,8,2,2,128]{5,1,4,2,3,0:T(8,128)(2,1)S(1)}, u32[]{:S(2)}, u32[]{:S(2)}) async-start(bf16[8,8,8,2,2,128]{5,1,4,2,3,0:T(8,128)(2,1)} %bitcast.147), calls=%async_computation.4 | async-start | bytes 1048576 | tf_op jit(solution)/shard_map/all_to_all | solution.py:188
  134.7 18.3 %all-to-all-start.5 = ((bf16[8,8,8,2,2,128]{5,1,4,2,3,0:T(8,128)(2,1)}), bf16[8,8,8,2,2,128]{5,1,4,2,3,0:T(8,128)(2,1)S(1)}, u32[]{:S(2)}, u32[]{:S(2)}) async-start(bf16[8,8,8,2,2,128]{5,1,4,2,3,0:T(8,128)(2,1)} %bitcast.146), calls=%async_computation.5 | async-start | bytes 1048576 | tf_op jit(solution)/shard_map/all_to_all | solution.py:188
  140.3 13.6 %collective-permute-start.4 = (bf16[8,2,8,16,128]{4,0,1,3,2:T(8,128)(2,1)S(1)}, bf16[8,2,8,16,128]{4,0,1,3,2:T(8,128)(2,1)S(1)}, u32[]{:S(2)}, u32[]{:S(2)}) collective-permute-start(bf16[8,2,8,16,128]{4,0,1,3,2:T(8,128)(2,1)S(1)} %bitcast.160), channel_id=1, source_target_pairs={{0,2},{1,3},{2,0},{3,1},{4,6},{5,7},{6,4},{7,5},{8,10},{9,11},{10,... | collective-permute-start | bytes 1572872 | tf_op jit(solution)/shard_map/ppermute | solution.py:148
  153.1 14.9 %copy-start.3 = (bf16[128]{0:T(256)(128)(2,1)S(1)}, bf16[128]{0:T(256)(128)(2,1)}, u32[]{:S(2)}) copy-start(bf16[128]{0:T(256)(128)(2,1)} %param.11) | copy-start | bytes 772
  153.1 13.1 %collective-permute-start.6 = (bf16[8,2,8,16,128]{4,0,1,3,2:T(8,128)(2,1)S(1)}, bf16[8,2,8,16,128]{4,0,1,3,2:T(8,128)(2,1)S(1)}, u32[]{:S(2)}, u32[]{:S(2)}) collective-permute-start(bf16[8,2,8,16,128]{4,0,1,3,2:T(8,128)(2,1)S(1)} %bitcast.163), channel_id=1, source_target_pairs={{0,2},{1,3},{2,0},{3,1},{4,6},{5,7},{6,4},{7,5},{8,10},{9,11},{10,... | collective-permute-start | bytes 1572872 | tf_op jit(solution)/shard_map/ppermute | solution.py:148
  155.0 13.0 %collective-permute-start.5 = (bf16[16,2,8,16,128]{4,0,1,3,2:T(8,128)(2,1)}, bf16[16,2,8,16,128]{4,0,1,3,2:T(8,128)(2,1)}, u32[]{:S(2)}, u32[]{:S(2)}) collective-permute-start(bf16[16,2,8,16,128]{4,0,1,3,2:T(8,128)(2,1)} %pad_maximum_fusion.1), channel_id=1, source_target_pairs={{0,1},{1,0},{2,3},{3,2},{4,5},{5,4},{6,7},{7,6},{8,9},{9,8},{10,11... | collective-permute-start | bytes 3145736 | tf_op jit(solution)/shard_map/ppermute | solution.py:148
  166.4 4.5 %collective-permute-start.7 = (bf16[16,2,8,16,128]{4,0,1,3,2:T(8,128)(2,1)S(1)}, bf16[16,2,8,16,128]{4,0,1,3,2:T(8,128)(2,1)}, u32[]{:S(2)}, u32[]{:S(2)}) collective-permute-start(bf16[16,2,8,16,128]{4,0,1,3,2:T(8,128)(2,1)S(1)} %pad_maximum_fusion.2), channel_id=1, source_target_pairs={{0,1},{1,0},{2,3},{3,2},{4,5},{5,4},{6,7},{7,6},{8,9},{9,8},{10,11... | collective-permute-start | bytes 3145736 | tf_op jit(solution)/shard_map/ppermute | solution.py:148
  172.9 0.8 copy-start
where the time goes:
time: 237 us; the launch traced here: 233 us
  Pallas kernels  78.2 us (33%)
  waiting for transfers between devices  77.4 us (33%)
  starting transfers between devices  38.4 us (16%)
  matrix products  22.5 us (9%)
  local copies, waits for them, and re-layouts  10.9 us (5%)
  other arithmetic  5.58 us (2%)
    pallas_call x2, Pallas kernels, finish(): pl.pallas_call(final_body, grid=(count, rows // block), in_specs=in_specs...  59.6 us
    ppermute x8, waiting for transfers between devices, swap(): return lax.ppermute(value, 'ba', [(i, i ^ 1 << bit) for i in range(n_ba)])  32.5 us
    all_to_all x2, waiting for transfers between devices, per_device(): piece = lax.all_to_all(back[:, ch], 'aa', 0, 0, tiled=True)  23.7 us
    pallas_call x2, Pallas kernels, depth_forward(): pl.pallas_call(depth_body, grid=(count,), in_specs=[pl.BlockSpec((modes,...  18.6 us
    all_to_all x2, waiting for transfers between devices, per_device(): landed.append(lax.all_to_all(part, 'aa', 0, 0, tiled=True))  11.4 us
    all_to_all x2, starting transfers between devices, per_device(): piece = lax.all_to_all(back[:, ch], 'aa', 0, 0, tiled=True)  10.9 us
    all_to_all x2, starting transfers between devices, per_device(): landed.append(lax.all_to_all(part, 'aa', 0, 0, tiled=True))  10.9 us
    dot_general x1, matrix products, per_device(): by_real = jnp.einsum(pattern, spec, weight_real, preferred_element_type=F32)  8.05 us
  transfers between devices with their start and end apart: 14, of which 8 were waited for; matrix products, arithmetic and copies ran while one was open for 5% of the time, Pallas kernels for 4%

commit v1 on v0

v1 whole, which is shorter than its diff:
```python
import functools
import math

import jax
import jax.numpy as jnp
import numpy as np
from jax import lax
from jax.experimental import pallas as pl
from jax.experimental.pallas import tpu as pltpu
from jax.sharding import PartitionSpec as P

BF = jnp.bfloat16
F32 = jnp.float32
MESH = pl.DeviceIdType.MESH


def kept_modes(length, number, positions):
    return np.where(positions < number // 2, positions, positions + (length - number))


def phase_tables(length, places, mode_list):
    phase_steps = places[:, None] * mode_list[None, :] % length
    angles = phase_steps.astype(np.float32) * np.float32(2.0 * math.pi / length)
    return np.cos(angles), np.sin(angles)


def forward_table(length, places, modes):
    c, s = phase_tables(length, places, modes)
    return np.stack([np.stack([c, -s], 1), np.stack([s, c], 1)], 0)


def inverse_table(length, places, modes):
    c, s = phase_tables(length, places, modes)
    c, s = c.T, s.T
    return np.stack([np.stack([c, s], 1), np.stack([-s, c], 1)], 0)


def spectral_body(
    n_aa, n_ba, halves, parts, slots,
    depth_ref, y_ref, x_fwd_ref, x_inv_ref, keep_ref, x_ref, wr_ref, wi_ref,
    out_ref,
    xbuf, wbuf, lines, plane, sends, gots, outgo, landed, spec_out, spec_in,
    mix_out, mix_in, back,
    x_sem, w_sem, rs_send, rs_recv, fa_send, fa_recv, ba_send, ba_recv,
    ia_send, ia_recv, ag_send, ag_recv,
):
    n_x, n_y, depth, chans = x_ref.shape
    kx_own, ky, kz_own = wr_ref.shape[:3]
    kz = kz_own * n_aa
    ky_own = ky // n_ba
    q_part = ky_own // parts
    bits = n_ba.bit_length() - 1
    x_half = n_x // halves
    rows2 = 2 * x_half
    me_a = lax.axis_index("aa")
    me_b = lax.axis_index("ba")

    barrier = pltpu.get_barrier_semaphore()
    for d in range(1, n_aa):
        pl.semaphore_signal(barrier, inc=1, device_id=((me_a + d) % n_aa, me_b), device_id_type=MESH)
    for d in range(1, n_ba):
        pl.semaphore_signal(barrier, inc=1, device_id=(me_a, (me_b + d) % n_ba), device_id_type=MESH)

    def fetch(i):
        return pltpu.make_async_copy(x_ref.at[i], xbuf.at[i % slots], x_sem.at[i % slots])

    for i in range(slots):
        fetch(i).start()

    stride = lines.shape[0] // (2 * kz)

    def row(i, carry):
        fetch(i).wait()
        slot = i % slots
        for j in range(0, n_y, 2):
            pair = jnp.concatenate([xbuf[slot, j], xbuf[slot, j + 1]], axis=1)
            res = jnp.dot(depth_ref[...], pair, preferred_element_type=F32)
            for u in range(2):
                for g in range(2 * kz // 8):
                    lines[pl.ds(8 * g * stride + j + u, 8, stride=stride), :] = res[
                        8 * g : 8 * g + 8, u * chans : (u + 1) * chans
                    ]

        @pl.when(i + slots < n_x)
        def _():
            fetch(i + slots).start()

        half = i // x_half
        local = i % x_half
        for k in range(0, kz, 2):
            cols = []
            for kk in (k, k + 1):
                re = lines[kk * stride : kk * stride + n_y, :]
                im = lines[(kz + kk) * stride : (kz + kk) * stride + n_y, :]
                cols.append(jnp.concatenate([re, im], axis=0).astype(BF))
            res = jnp.dot(y_ref[...], jnp.concatenate(cols, axis=1), preferred_element_type=F32)
            for u in range(2):
                for g in range(2 * ky // 8):
                    start = (k + u) * 2 * ky * x_half + 8 * g * x_half + local
                    plane[half, pl.ds(start, 8, stride=x_half), :] = res[
                        8 * g : 8 * g + 8, u * chans : (u + 1) * chans
                    ]
        return carry

    def partner(bit):
        return (me_a, me_b ^ (1 << bit))

    def chunk_sum(h, c, blk, k, q, upto):
        base = ((k * n_ba + blk) * parts + c) * q_part + q
        total = plane[h, pl.ds(base * rows2, rows2), :]
        for t in range(upto):
            total = total + gots[t][h * parts + c, blk, k, q].astype(F32)
        return total

    def rs_copy(s, g):
        return pltpu.make_async_remote_copy(
            src_ref=sends[s].at[g], dst_ref=gots[s].at[g],
            send_sem=rs_send.at[s, g], recv_sem=rs_recv.at[s, g],
            device_id=partner(s), device_id_type=MESH,
        )

    def rs_step(s, h, c):
        g = h * parts + c
        if s > 0:
            rs_copy(s - 1, g).wait_recv()
        left = n_ba >> (s + 1)

        def one(k, carry):
            for blk in range(left):
                for q in range(q_part):
                    sends[s][g, blk, k, q] = chunk_sum(h, c, left + blk, k, q, s).astype(BF)
            return carry

        lax.fori_loop(0, kz, one, 0)
        rs_copy(s, g).start()

    def fa_copy(g, d):
        peer = (me_a + d) % n_aa
        return pltpu.make_async_remote_copy(
            src_ref=outgo.at[g, peer], dst_ref=landed.at[g, me_a],
            send_sem=fa_send.at[g, d], recv_sem=fa_recv.at[g, d],
            device_id=(peer, me_b), device_id_type=MESH,
        )

    def fa_step(h, c):
        g = h * parts + c
        rs_copy(bits - 1, g).wait_recv()

        def one(a, carry):
            for kk in range(kz_own):
                for q in range(q_part):
                    outgo[g, a, kk, q] = chunk_sum(h, c, 0, a * kz_own + kk, q, bits).astype(BF)
            return carry

        lax.fori_loop(0, n_aa, one, 0)
        for d in range(1, n_aa):
            fa_copy(g, d).start()
        landed[g, me_a] = outgo[g, me_a]

    def weight_fetch(p, m):
        ref = (wr_ref, wi_ref)[p]
        return pltpu.make_async_copy(ref.at[m], wbuf.at[p, m], w_sem.at[p, m])

    everything = [(h, c) for h in range(halves) for c in range(parts)]

    lax.fori_loop(0, x_half, row, 0)
    pl.semaphore_wait(barrier, n_aa + n_ba - 2)
    for c in range(parts):
        rs_step(0, 0, c)
    for h in range(1, halves):
        first = h * x_half
        lax.fori_loop(first, first + 2, row, 0)
        for c in range(parts):
            rs_step(1, h - 1, c)
        lax.fori_loop(first + 2, first + x_half, row, 0)
        for c in range(parts):
            rs_step(0, h, c)
    for p in range(2):
        for m in range(kx_own):
            weight_fetch(p, m).start()
    for s in range(1, bits):
        for h, c in everything:
            if s > 1 or h == halves - 1:
                rs_step(s, h, c)
    for h, c in everything:
        fa_step(h, c)

    def ba_copy(which, d):
        peer = (me_b + d) % n_ba
        src, dst = ((spec_out, spec_in), (mix_out, mix_in))[which]
        return pltpu.make_async_remote_copy(
            src_ref=src.at[peer], dst_ref=dst.at[me_b],
            send_sem=ba_send.at[which, d], recv_sem=ba_recv.at[which, d],
            device_id=(me_a, peer), device_id_type=MESH,
        )

    own2 = 2 * kx_own
    for c in range(parts):
        for h in range(halves):
            for d in range(1, n_aa):
                fa_copy(h * parts + c, d).wait_recv()
        for kk in range(kz_own):
            for q in range(0, q_part, 2):
                cols = []
                for qq in (q, q + 1):
                    cols.append(jnp.concatenate(
                        [landed[h * parts + c, a, kk, qq] for h in range(halves) for a in range(n_aa)], axis=0
                    ))
                res = jnp.dot(x_fwd_ref[...], jnp.concatenate(cols, axis=1), preferred_element_type=F32)
                for u in range(2):
                    for b in range(n_ba):
                        spec_out[b, kk, c * q_part + q + u] = res[
                            b * own2 : (b + 1) * own2, u * chans : (u + 1) * chans
                        ].astype(BF)
    for d in range(1, n_ba):
        ba_copy(0, d).start()
    spec_in[me_b] = spec_out[me_b]
    for p in range(2):
        for m in range(kx_own):
            weight_fetch(p, m).wait()
    for d in range(1, n_ba):
        ba_copy(0, d).wait_recv()

    place = lax.broadcasted_iota(jnp.int32, (own2, chans), 0) % kx_own

    def mix(j, carry):
        b = j // ky_own
        q = j % ky_own
        level = jnp.where(j < ky // 2, j, ky - 1 - j)
        for kk in range(kz_own):
            val = spec_in[b, kk, q].astype(F32)
            turned = jnp.concatenate([-val[kx_own:], val[:kx_own]], axis=0)
            lhs = jnp.concatenate([val, turned], axis=1).astype(BF)
            total = jnp.zeros((own2, chans), F32)
            for m in range(0, kx_own, 2):
                cols = [
                    jnp.concatenate([wbuf[0, mm, j, kk], wbuf[1, mm, j, kk]], axis=0) for mm in (m, m + 1)
                ]
                res = jnp.dot(lhs, jnp.concatenate(cols, axis=1), preferred_element_type=F32)
                total = jnp.where(place == m, res[:, :chans], total)
                total = jnp.where(place == m + 1, res[:, chans:], total)
            total = jnp.where(level < keep_ref[kk], total, 0.0)
            mix_out[b, q, kk] = total.astype(BF)
        return carry

    lax.fori_loop(0, ky, mix, 0)
    for d in range(1, n_ba):
        ba_copy(1, d).start()
    mix_in[me_b] = mix_out[me_b]
    for d in range(1, n_ba):
        ba_copy(1, d).wait_recv()

    def ia_copy(g, d):
        peer = (me_a + d) % n_aa
        return pltpu.make_async_remote_copy(
            src_ref=back.at[g, peer], dst_ref=out_ref.at[g, 0, me_a],
            send_sem=ia_send.at[g, d], recv_sem=ia_recv.at[g, d],
            device_id=(peer, me_b), device_id_type=MESH,
        )

    for c in range(parts):
        for kk in range(kz_own):
            for q in range(0, q_part, 2):
                cols = []
                for qq in (c * q_part + q, c * q_part + q + 1):
                    cols.append(jnp.concatenate(
                        [mix_in[b, qq, kk].astype(F32) for b in range(n_ba)], axis=0
                    ).astype(BF))
                res = jnp.dot(x_inv_ref[...], jnp.concatenate(cols, axis=1), preferred_element_type=F32)
                for u in range(2):
                    for h in range(halves):
                        for a in range(n_aa):
                            first = (h * n_aa + a) * rows2
                            back[h * parts + c, a, kk, q + u] = res[
                                first : first + rows2, u * chans : (u + 1) * chans
                            ].astype(BF)
        for h in range(halves):
            for d in range(1, n_aa):
                ia_copy(h * parts + c, d).start()
            out_ref[h * parts + c, 0, me_a] = back[h * parts + c, me_a]

    order = [h * parts + c for c in range(parts) for h in range(halves)]

    def ag_copy(t, g):
        n = 1 << (bits - 1 - t)
        return pltpu.make_async_remote_copy(
            src_ref=out_ref.at[g, pl.ds(0, n)], dst_ref=out_ref.at[g, pl.ds(n, n)],
            send_sem=ag_send.at[t, g], recv_sem=ag_recv.at[t, g],
            device_id=partner(t), device_id_type=MESH,
        )

    steps = list(reversed(range(bits)))
    total_chunks = len(order)
    for tick in range(total_chunks + bits - 1):
        for n, t in enumerate(steps):
            pos = tick - n
            if 0 <= pos < total_chunks:
                g = order[pos]
                if n == 0:
                    for d in range(1, n_aa):
                        ia_copy(g, d).wait_recv()
                else:
                    ag_copy(steps[n - 1], g).wait_recv()
                ag_copy(t, g).start()
    for g in order:
        ag_copy(steps[-1], g).wait_recv()

    for g in range(halves * parts):
        for s in range(bits):
            rs_copy(s, g).wait_send()
            ag_copy(s, g).wait_send()
        for d in range(1, n_aa):
            fa_copy(g, d).wait_send()
            ia_copy(g, d).wait_send()
    for which in range(2):
        for d in range(1, n_ba):
            ba_copy(which, d).wait_send()


def spectral(n_aa, n_ba, halves, parts, grid_features, weight_real, weight_imag, tables):
    n_x, n_y, depth, chans = grid_features.shape
    kx_own, ky, kz_own = weight_real.shape[:3]
    kz = kz_own * n_aa
    ky_own = ky // n_ba
    q_part = ky_own // parts
    bits = n_ba.bit_length() - 1
    rows2 = 2 * n_x // halves
    chunks = halves * parts
    slots = 4
    stride = n_y + 8
    vm = pltpu.VMEM
    dma = pltpu.SemaphoreType.DMA

    def rs_shape(s):
        left = n_ba >> (s + 1)
        return vm((chunks, left, kz, q_part, rows2, chans), BF)

    inner = pl.BlockSpec(memory_space=pltpu.VMEM)
    outer = pl.BlockSpec(memory_space=pl.ANY)
    return pl.pallas_call(
        functools.partial(spectral_body, n_aa, n_ba, halves, parts, slots),
        in_specs=[inner] * 5 + [outer] * 3,
        out_specs=inner,
        out_shape=jax.ShapeDtypeStruct((chunks, n_ba, n_aa, kz_own, q_part, rows2, chans), BF),
        scratch_shapes=[
            vm((slots, n_y, depth, chans), BF),
            vm((2,) + weight_real.shape, BF),
            vm((2 * kz * stride, chans), F32),
            vm((halves, kz * 2 * ky * (n_x // halves), chans), F32),
            [rs_shape(t) for t in range(bits)], [rs_shape(t) for t in range(bits)],
            vm((chunks, n_aa, kz_own, q_part, rows2, chans), BF),
            vm((chunks, n_aa, kz_own, q_part, rows2, chans), BF),
            vm((n_ba, kz_own, ky_own, 2 * kx_own, chans), BF),
            vm((n_ba, kz_own, ky_own, 2 * kx_own, chans), BF),
            vm((n_ba, ky_own, kz_own, 2 * kx_own, chans), BF),
            vm((n_ba, ky_own, kz_own, 2 * kx_own, chans), BF),
            vm((chunks, n_aa, kz_own, q_part, rows2, chans), BF),
            dma((slots,)), dma((2, kx_own)),
            dma((bits, chunks)), dma((bits, chunks)),
            dma((chunks, n_aa)), dma((chunks, n_aa)),
            dma((2, n_ba)), dma((2, n_ba)),
            dma((chunks, n_aa)), dma((chunks, n_aa)),
            dma((bits, chunks)), dma((bits, chunks)),
        ],
        compiler_params=pltpu.CompilerParams(
            collective_id=0, has_side_effects=True, vmem_limit_bytes=67043328
        ),
    )(*tables, grid_features, weight_real, weight_imag)


def final_body(slots, table_ref, w_ref, bias_ref, back_ref, x_ref, out_ref, xbuf, obuf, in_sem, out_sem):
    n_x = x_ref.shape[0]
    n_y = x_ref.shape[1]
    c1 = 2.0 * math.sqrt(2.0 / math.pi)

    def fetch(i):
        return pltpu.make_async_copy(x_ref.at[i], xbuf.at[i % slots], in_sem.at[i % slots])

    def flush(i):
        return pltpu.make_async_copy(obuf.at[i % slots], out_ref.at[i], out_sem.at[i % slots])

    for i in range(slots):
        fetch(i).start()

    def step(i, carry):
        fetch(i).wait()

        @pl.when(i >= slots)
        def _():
            flush(i - slots).wait()

        slot = i % slots
        for j in range(n_y):
            lhs = jnp.concatenate([xbuf[slot, j], table_ref[...]], axis=1)
            rhs = jnp.concatenate([w_ref[...], back_ref[i, j], bias_ref[...]], axis=0)
            half = jnp.dot(lhs, rhs, preferred_element_type=F32)
            inner = half * (c1 + (4.0 * c1 * 0.044715) * (half * half))
            obuf[slot, j] = (half + half * jnp.tanh(inner)).astype(BF)
        flush(i).start()

        @pl.when(i + slots < n_x)
        def _():
            fetch(i + slots).start()

        return carry

    lax.fori_loop(0, n_x, step, 0)
    for i in range(n_x - slots, n_x):
        flush(i).wait()


def finish(grid_features, back, table, weight, bias):
    n_x, n_y, depth, chans = grid_features.shape
    modes = back.shape[2]
    extra = 16
    column = (np.arange(extra) == 0).astype(np.float32)
    table = np.concatenate([table.astype(np.float32), np.broadcast_to(column, (depth, extra))], axis=1)
    table = jnp.asarray((0.5 * table).astype(BF))
    weight = (0.5 * weight.astype(F32)).astype(BF)
    bias = (bias.astype(F32)[None, :] * column[:, None]).astype(BF)
    slots = 3
    inner = pl.BlockSpec(memory_space=pltpu.VMEM)
    outer = pl.BlockSpec(memory_space=pl.ANY)
    return pl.pallas_call(
        functools.partial(final_body, slots),
        in_specs=[inner] * 4 + [outer],
        out_specs=outer,
        out_shape=jax.ShapeDtypeStruct(grid_features.shape, BF),
        scratch_shapes=[
            pltpu.VMEM((slots, n_y, depth, chans), BF),
            pltpu.VMEM((slots, n_y, depth, chans), BF),
            pltpu.SemaphoreType.DMA((slots,)),
            pltpu.SemaphoreType.DMA((slots,)),
        ],
        compiler_params=pltpu.CompilerParams(vmem_limit_bytes=32 << 20),
        cost_estimate=pl.CostEstimate(
            flops=2 * n_x * n_y * depth * chans * (chans + modes),
            bytes_accessed=4 * n_x * n_y * depth * chans,
            transcendentals=n_x * n_y * depth * chans,
        ),
    )(table, weight, bias, back, grid_features)


def per_device(
    n_aa, n_ba, grid_features, weight_real, weight_imag, mode_keep, local_weight, local_bias
):
    n_x, n_y, depth, chans = grid_features.shape
    kx_own, ky, kz_own = weight_real.shape[:3]
    nx, ny = n_x * n_aa, n_y * n_ba
    kx, kz, ky_own = kx_own * n_ba, kz_own * n_aa, ky // n_ba
    bits = n_ba.bit_length() - 1
    me = lax.axis_index("ba")
    halves = max(n_x // 8, 1)
    parts = max(min(2, ky_own // 2), 1)
    x_half, q_part = n_x // halves, ky_own // parts

    c, s = phase_tables(depth, np.arange(depth), np.arange(kz))
    depth_fwd = np.concatenate([c, -s], axis=1).T.astype(BF)
    factor = np.where(np.arange(kz) == 0, 1.0, 2.0).astype(np.float32) / (nx * ny * depth)
    depth_inv = np.concatenate([c * factor, -s * factor], axis=1).astype(BF)

    y_fwd, y_inv = [], []
    order = np.arange(n_ba)
    block = np.zeros_like(order)
    for bit in range(bits):
        block = block + ((order >> (bits - 1 - bit)) & 1) * (1 << bit)
    for who in range(n_ba):
        ky_pos = ((block ^ who)[:, None] * ky_own + np.arange(ky_own)[None, :]).reshape(-1)
        ky_modes = kept_modes(ny, ky, ky_pos)
        own_y = who * n_y + np.arange(n_y)
        table = forward_table(ny, own_y, ky_modes)
        y_fwd.append(np.transpose(table, (3, 2, 0, 1)).reshape(2 * ky, 2 * n_y).astype(BF))
        y_inv.append(inverse_table(ny, own_y, ky_modes).astype(BF))
    y_fwd = jnp.asarray(np.stack(y_fwd))[me]
    y_inv = jnp.asarray(np.stack(y_inv))[me]
    x_modes = kept_modes(nx, kx, np.arange(kx))
    x_fwd = forward_table(nx, np.arange(nx), x_modes)
    x_fwd = x_fwd.reshape(2, n_aa, halves, x_half, 2, n_ba, kx_own)
    x_fwd = np.transpose(x_fwd, (5, 4, 6, 2, 1, 0, 3)).reshape(2 * kx, 2 * nx).astype(BF)
    x_inv = inverse_table(nx, np.arange(nx), x_modes)
    x_inv = x_inv.reshape(2, n_ba, kx_own, 2, n_aa, halves, x_half)
    x_inv = np.transpose(x_inv, (5, 4, 3, 6, 1, 0, 2)).reshape(2 * nx, 2 * kx).astype(BF)
    keep = jnp.concatenate([mode_keep.T, mode_keep.T], axis=1)
    keep = jnp.broadcast_to(keep[:, :, None], (kz_own, 2 * kx_own, chans))

    field = spectral(
        n_aa, n_ba, halves, parts, grid_features, weight_real, weight_imag,
        (depth_fwd, y_fwd, x_fwd, x_inv, keep),
    )
    field = field.reshape(halves, parts, n_ba, n_aa, kz_own, q_part, 2, x_half, chans)
    y_inv = y_inv.reshape(2, n_ba, parts, q_part, 2, n_y)
    back = jnp.einsum("hsbakqpxc,pbsqry->hxyrakc", field, y_inv, preferred_element_type=F32)
    back = back.astype(BF).reshape(n_x, n_y, 2 * kz, chans)
    return finish(grid_features, back, depth_inv, local_weight, local_bias)


def solution(mesh):
    in_specs = (
        P("aa", "ba", None, None),
        P("ba", None, "aa", None, None),
        P("ba", None, "aa", None, None),
        P("ba", "aa"),
        P(),
        P(),
    )
    out_specs = P("aa", "ba", None, None)
    body = functools.partial(per_device, mesh.shape["aa"], mesh.shape["ba"])
    return jax.shard_map(body, mesh=mesh, in_specs=in_specs, out_specs=out_specs, check_vma=False)
```

time: 237 us -> 147 us (0.62); the launches traced: 233 us -> 147 us
  waiting for transfers between devices: 77.4 us -> 0 us
  Pallas kernels: 78.2 us -> 125 us
  starting transfers between devices: 38.4 us -> 0 us
  matrix products: 22.5 us -> 7.62 us
    pallas_call x4 -> x2, Pallas kernels: 78.2 us -> 125 us  [the longest x1 101 us: spectral(): pl.pallas_call(functools.partial(spectral_body, n_aa, n_ba, halves, parts...]
    all_to_all x6 -> x0, waiting for transfers between devices: 44.9 us -> none  [the longest x2 23.7 us: per_device(): piece = lax.all_to_all(back[:, ch], 'aa', 0, 0, tiled=True)]
    ppermute x8 -> x0, waiting for transfers between devices: 32.5 us -> none  [swap(): return lax.ppermute(value, 'ba', [(i, i ^ 1 << bit) for i in range(n_ba)])]
    all_to_all x6 -> x0, starting transfers between devices: 31.3 us -> none  [the longest x2 10.9 us: per_device(): piece = lax.all_to_all(back[:, ch], 'aa', 0, 0, tiled=True)]
    dot_general x8 -> x1, matrix products: 22.5 us -> 7.62 us  [per_device(): jnp.einsum('hsbakqpxc,pbsqry->hxyrakc', field, y_inv, preferred_element_t...]
    ppermute x8 -> x0, starting transfers between devices: 7.11 us -> none  [swap(): return lax.ppermute(value, 'ba', [(i, i ^ 1 << bit) for i in range(n_ba)])]
    convert_element_type x2 -> x1, local copies, waits for them, and re-layouts: 1.63 us -> 6.53 us  [per_device(): back = back.astype(BF).reshape(n_x, n_y, 2 * kz, chans)]
    unnamed x11 -> x6, local copies, waits for them, and re-layouts: 3.98 us -> 0.01 us
  transfers between devices with their start and end apart: 14 -> 0, of which waited for: 8 -> 0; matrix products, arithmetic and copies ran while one was open for 5% -> 0% of each run, Pallas kernels for 4% -> 0%
where the time goes in v1:
time: 147 us
  Pallas kernels  125 us (85%)
  local copies, waits for them, and re-layouts  9.9 us (7%)
  matrix products  7.62 us (5%)
  other arithmetic  4.18 us (3%)
    pallas_call x1, Pallas kernels, spectral(): pl.pallas_call(functools.partial(spectral_body, n_aa, n_ba, halves, parts...  101 us
    pallas_call x1, Pallas kernels, finish(): pl.pallas_call(functools.partial(final_body, slots), in_specs=[inner] * 4...  24.3 us
    dot_general x1, matrix products, per_device(): jnp.einsum('hsbakqpxc,pbsqry->hxyrakc', field, y_inv, preferred_element_t...  7.62 us
    convert_element_type x1, local copies, waits for them, and re-layouts, per_device(): back = back.astype(BF).reshape(n_x, n_y, 2 * kz, chans)  6.53 us

profile of v1, /device:TPU:27, one launch (start us, length us, event | category | flops | bytes accessed | tf_op | source)
XLA Modules:
  0.0 146.6 jit_solution(4877123152438267003)
XLA Ops:
  0.0 0.7 convert_element_type.20
  0.7 0.8 pad_add_fusion
  1.5 1.3 multiply_convert_fusion.1.bias_ref
  2.8 0.7 broadcast_in_dim.2.keep_ref
  3.5 1.3 dynamic-slice_bitcast_fusion.y_ref
  4.8 1.4 constant_dynamic-slice_fusion
  6.2 1.4 multiply_convert_fusion.w_ref
  7.5 100.6 %shard_map.127 = bf16[4,4,8,2,4,16,128]{6,5,4,3,2,1,0:T(8,128)(2,1)} custom-call(bf16[32,256]{1,0:T(8,128)(2,1)} %constant.26.clone.depth_ref, bf16[64,64]{1,0:T(8,128)(2,1)} %dynamic-slice_bitcast_fusion.y_ref, bf16[64,256]{1,0:T(8,128)(2,1)} %constant.27.clone.x_fwd_ref, bf16[256,64]{1,0:T(8,128)(2,1)} %constant.28.clone.x_inv_ref, ...), custom_call_target="tpu_custom_call" | custom-call | tf_op jit(solution)/shard_map/pallas_call | solution.py:340
  108.1 7.6 %fusion = bf16[2,8,32,2,8,2,128]{6,2,1,5,4,0,3:T(8,128)(2,1)} fusion(bf16[2,2,4,8,2,4,2,8,128]{8,7,6,5,4,3,2,1,0:T(8,128)(2,1)} %bitcast.22, bf16[2,4,2,4,2,32,1,1,1,1]{5,3,2,1,4,0,9,8,7,6:T(4,128)(2,1)} %bitcast.23), kind=kOutput, calls=%fused_computation.1 | convolution fusion | flops 270532608 | bytes 8396800 | tf_op jit(solution)/shard_map/hsbakqpxc,pbsqry->hxyrakc/dot_general | solution.py:492
  115.7 0.0 copy-start
  115.7 0.0 copy-start.1
  115.7 0.0 copy-start.2
  115.7 6.5 %copy.18 = bf16[2,8,32,2,8,2,128]{6,5,4,3,2,1,0:T(2,128)(2,1)S(1)} copy(bf16[2,8,32,2,8,2,128]{6,2,1,5,4,0,3:T(8,128)(2,1)} %fusion) | data formatting | bytes 8388608 | tf_op jit(solution)/shard_map/convert_element_type | solution.py:493
  122.3 0.0 copy-done
  122.3 0.0 copy-done.1
  122.3 0.0 copy-done.2
  122.3 24.3 %shard_map.128 = bf16[16,32,256,128]{3,2,1,0:T(8,128)(2,1)} custom-call(bf16[256,48]{1,0:T(8,128)(2,1)S(1)} %copy-done.1, bf16[128,128]{1,0:T(8,128)(2,1)S(1)} %copy-done, bf16[16,128]{1,0:T(8,128)(2,1)S(1)} %copy-done.2, bf16[16,32,32,128]{3,2,1,0:T(8,128)(2,1)S(1)} %bitcast.21, bf16[16,32,256,128]{3,2,1,0:T(8,128)(2,1)} %x_ref.3), custom_call_target="tpu_custom_call" | custom-call | flops 5368709120 | bytes 67108864 | tf_op jit(solution)/shard_map/pallas_call | solution.py:424
Async XLA Ops:
  115.7 6.5 %copy-start = (bf16[128,128]{1,0:T(8,128)(2,1)S(1)}, bf16[128,128]{1,0:T(8,128)(2,1)}, u32[]{:S(2)}) copy-start(bf16[128,128]{1,0:T(8,128)(2,1)} %multiply_convert_fusion.w_ref) | copy-start | bytes 98308
  115.7 6.6 %copy-start.1 = (bf16[256,48]{1,0:T(8,128)(2,1)S(1)}, bf16[256,48]{1,0:T(8,128)(2,1)}, u32[]{:S(2)}) copy-start(bf16[256,48]{1,0:T(8,128)(2,1)} %constant.29.clone.table_ref) | copy-start | bytes 73732
  115.7 6.6 %copy-start.2 = (bf16[16,128]{1,0:T(8,128)(2,1)S(1)}, bf16[16,128]{1,0:T(8,128)(2,1)}, u32[]{:S(2)}) copy-start(bf16[16,128]{1,0:T(8,128)(2,1)} %multiply_convert_fusion.1.bias_ref) | copy-start | bytes 12292

commit v2 on v1

v2 whole, which is shorter than its diff:
```python
import functools
import math

import jax
import jax.numpy as jnp
import numpy as np
from jax import lax
from jax.experimental import pallas as pl
from jax.experimental.pallas import tpu as pltpu
from jax.sharding import PartitionSpec as P

BF = jnp.bfloat16
F32 = jnp.float32
MESH = pl.DeviceIdType.MESH


def kept_modes(length, number, positions):
    return np.where(positions < number // 2, positions, positions + (length - number))


def phase_tables(length, places, mode_list):
    phase_steps = places[:, None] * mode_list[None, :] % length
    angles = phase_steps.astype(np.float32) * np.float32(2.0 * math.pi / length)
    return np.cos(angles), np.sin(angles)


def forward_table(length, places, modes):
    c, s = phase_tables(length, places, modes)
    return np.stack([np.stack([c, -s], 1), np.stack([s, c], 1)], 0)


def inverse_table(length, places, modes):
    c, s = phase_tables(length, places, modes)
    c, s = c.T, s.T
    return np.stack([np.stack([c, s], 1), np.stack([-s, c], 1)], 0)


def spectral_body(
    n_aa, n_ba, halves, parts, slots,
    depth_in, y_in, y_inv_in, x_fwd_in, x_inv_in, keep_in, x_ref, wr_ref, wi_ref,
    out_ref,
    depth_ref, y_ref, y_inv_ref, x_fwd_ref, x_inv_ref, keep_ref, kept_rows,
    xbuf, wbuf, lines, plane, sends, gots, outgo, landed, spec_out, spec_in,
    mix_out, mix_in, back, field,
    x_sem, w_sem, rs_send, rs_recv, fa_send, fa_recv, ba_send, ba_recv,
    ia_send, ia_recv, ag_send, ag_recv, o_sem, t_sem,
):
    n_x, n_y, depth, chans = x_ref.shape
    kx_own, ky, kz_own = wr_ref.shape[:3]
    kz = kz_own * n_aa
    ky_own = ky // n_ba
    q_part = ky_own // parts
    bits = n_ba.bit_length() - 1
    x_half = n_x // halves
    rows2 = 2 * x_half
    me_a = lax.axis_index("aa")
    me_b = lax.axis_index("ba")

    barrier = pltpu.get_barrier_semaphore()
    for d in range(1, n_aa):
        pl.semaphore_signal(barrier, inc=1, device_id=((me_a + d) % n_aa, me_b), device_id_type=MESH)
    for d in range(1, n_ba):
        pl.semaphore_signal(barrier, inc=1, device_id=(me_a, (me_b + d) % n_ba), device_id_type=MESH)

    def fetch(i):
        return pltpu.make_async_copy(x_ref.at[i], xbuf.at[i % slots], x_sem.at[i % slots])

    small = ((depth_in, depth_ref), (y_in, y_ref), (y_inv_in, y_inv_ref), (x_fwd_in, x_fwd_ref),
             (x_inv_in, x_inv_ref), (keep_in, keep_ref))
    tables = [pltpu.make_async_copy(src, dst, t_sem.at[n]) for n, (src, dst) in enumerate(small)]
    for copy in tables[:2]:
        copy.start()
    for i in range(slots):
        fetch(i).start()
    for copy in tables[2:]:
        copy.start()
    for copy in tables:
        copy.wait()
    own2 = 2 * kx_own
    place = lax.broadcasted_iota(jnp.int32, (own2, chans), 0) % kx_own
    for kk in range(kz_own):
        line = jnp.broadcast_to(keep_ref[kk : kk + 1, :].astype(F32), (own2, kx_own))
        spot = lax.broadcasted_iota(jnp.int32, (own2, kx_own), 0) % kx_own
        spot = spot == lax.broadcasted_iota(jnp.int32, (own2, kx_own), 1)
        kept_rows[kk] = jnp.broadcast_to(
            jnp.sum(jnp.where(spot, line, 0.0), axis=1, keepdims=True), (own2, chans)
        )

    stride = n_y + 8

    def depth_row(i, u2):
        fetch(i).wait()
        slot = i % slots
        for j in range(0, n_y, 2):
            pair = jnp.concatenate([xbuf[slot, j], xbuf[slot, j + 1]], axis=1)
            res = jnp.dot(depth_ref[...], pair, preferred_element_type=F32)
            for u in range(2):
                for g in range(2 * kz // 8):
                    lines[u2, pl.ds(8 * g * stride + j + u, 8, stride=stride), :] = res[
                        8 * g : 8 * g + 8, u * chans : (u + 1) * chans
                    ]

        @pl.when(i + slots < n_x)
        def _():
            fetch(i + slots).start()

    def y_row(i, u2):
        half = i // x_half
        local = i % x_half
        for k in range(0, kz, 2):
            cols = []
            for kk in (k, k + 1):
                re = lines[u2, kk * stride : kk * stride + n_y, :]
                im = lines[u2, (kz + kk) * stride : (kz + kk) * stride + n_y, :]
                cols.append(jnp.concatenate([re, im], axis=0).astype(BF))
            res = jnp.dot(y_ref[me_b], jnp.concatenate(cols, axis=1), preferred_element_type=F32)
            for u in range(2):
                for g in range(2 * ky // 8):
                    start = (k + u) * 2 * ky * x_half + 8 * g * x_half + local
                    plane[half, pl.ds(start, 8, stride=x_half), :] = res[
                        8 * g : 8 * g + 8, u * chans : (u + 1) * chans
                    ]

    def rows(t, carry):
        for u2 in range(2):
            depth_row(2 * t + u2, u2)
        for u2 in range(2):
            y_row(2 * t + u2, u2)
        return carry

    def partner(bit):
        return (me_a, me_b ^ (1 << bit))

    def chunk_sum(h, c, blk, k, q, upto):
        base = ((k * n_ba + blk) * parts + c) * q_part + q
        total = plane[h, pl.ds(base * rows2, rows2), :]
        for t in range(upto):
            total = total + gots[t][h * parts + c, blk, k, q].astype(F32)
        return total

    def rs_copy(s, g):
        return pltpu.make_async_remote_copy(
            src_ref=sends[s].at[g], dst_ref=gots[s].at[g],
            send_sem=rs_send.at[s, g], recv_sem=rs_recv.at[s, g],
            device_id=partner(s), device_id_type=MESH,
        )

    def rs_step(s, h, c):
        g = h * parts + c
        if s > 0:
            rs_copy(s - 1, g).wait_recv()
        left = n_ba >> (s + 1)

        def one(k, carry):
            for blk in range(left):
                for q in range(q_part):
                    sends[s][g, blk, k, q] = chunk_sum(h, c, left + blk, k, q, s).astype(BF)
            return carry

        lax.fori_loop(0, kz, one, 0)
        rs_copy(s, g).start()

    def fa_copy(g, d):
        peer = (me_a + d) % n_aa
        return pltpu.make_async_remote_copy(
            src_ref=outgo.at[g, peer], dst_ref=landed.at[g, me_a],
            send_sem=fa_send.at[g, d], recv_sem=fa_recv.at[g, d],
            device_id=(peer, me_b), device_id_type=MESH,
        )

    def fa_step(h, c):
        g = h * parts + c
        rs_copy(bits - 1, g).wait_recv()

        def one(a, carry):
            for kk in range(kz_own):
                for q in range(q_part):
                    outgo[g, a, kk, q] = chunk_sum(h, c, 0, a * kz_own + kk, q, bits).astype(BF)
            return carry

        lax.fori_loop(0, n_aa, one, 0)
        for d in range(1, n_aa):
            fa_copy(g, d).start()
        landed[g, me_a] = outgo[g, me_a]

    def weight_fetch(p, m):
        ref = (wr_ref, wi_ref)[p]
        return pltpu.make_async_copy(ref.at[m], wbuf.at[p, m], w_sem.at[p, m])

    steps_half = x_half // 2
    lax.fori_loop(0, steps_half, rows, 0)
    pl.semaphore_wait(barrier, n_aa + n_ba - 2)
    for c in range(parts):
        rs_step(0, 0, c)
    for h in range(1, halves):
        first = h * steps_half
        lax.fori_loop(first, first + 1, rows, 0)
        for c in range(parts):
            rs_step(1, h - 1, c)
        lax.fori_loop(first + 1, first + steps_half, rows, 0)
        for c in range(parts):
            rs_step(0, h, c)
    for p in range(2):
        for m in range(kx_own):
            weight_fetch(p, m).start()
    for c in range(parts):
        rs_step(1, halves - 1, c)
        for h in range(halves - 1):
            for s in range(2, bits):
                rs_step(s, h, c)
            fa_step(h, c)
    for c in range(parts):
        for s in range(2, bits):
            rs_step(s, halves - 1, c)
        fa_step(halves - 1, c)

    def ba_copy(which, c, d):
        peer = (me_b + d) % n_ba
        src, dst = ((spec_out, spec_in), (mix_out, mix_in))[which]
        return pltpu.make_async_remote_copy(
            src_ref=src.at[c, peer], dst_ref=dst.at[c, me_b],
            send_sem=ba_send.at[which, c, d], recv_sem=ba_recv.at[which, c, d],
            device_id=(me_a, peer), device_id_type=MESH,
        )

    def to_modes(c):
        for h in range(halves):
            for d in range(1, n_aa):
                fa_copy(h * parts + c, d).wait_recv()
        for kk in range(kz_own):
            for q in range(0, q_part, 2):
                cols = []
                for qq in (q, q + 1):
                    cols.append(jnp.concatenate(
                        [landed[h * parts + c, a, kk, qq] for h in range(halves) for a in range(n_aa)], axis=0
                    ))
                res = jnp.dot(x_fwd_ref[...], jnp.concatenate(cols, axis=1), preferred_element_type=F32)
                for u in range(2):
                    for b in range(n_ba):
                        spec_out[c, b, kk, q + u] = res[
                            b * own2 : (b + 1) * own2, u * chans : (u + 1) * chans
                        ].astype(BF)
        for d in range(1, n_ba):
            ba_copy(0, c, d).start()
        spec_in[c, me_b] = spec_out[c, me_b]

    def mix_modes(c):
        for d in range(1, n_ba):
            ba_copy(0, c, d).wait_recv()

        def mix(b, carry):
            for q in range(q_part):
                j = b * ky_own + c * q_part + q
                level = jnp.where(j < ky // 2, j, ky - 1 - j)
                for kk in range(kz_own):
                    val = spec_in[c, b, kk, q].astype(F32)
                    turned = jnp.concatenate([-val[kx_own:], val[:kx_own]], axis=0)
                    lhs = jnp.concatenate([val, turned], axis=1).astype(BF)
                    total = jnp.zeros((own2, chans), F32)
                    for m in range(0, kx_own, 2):
                        cols = [
                            jnp.concatenate([wbuf[0, mm, j, kk], wbuf[1, mm, j, kk]], axis=0)
                            for mm in (m, m + 1)
                        ]
                        res = jnp.dot(lhs, jnp.concatenate(cols, axis=1), preferred_element_type=F32)
                        total = jnp.where(place == m, res[:, :chans], total)
                        total = jnp.where(place == m + 1, res[:, chans:], total)
                    total = jnp.where(level.astype(F32) < kept_rows[kk], total, 0.0)
                    mix_out[c, b, q, kk] = total.astype(BF)
            return carry

        lax.fori_loop(0, n_ba, mix, 0)
        for d in range(1, n_ba):
            ba_copy(1, c, d).start()
        mix_in[c, me_b] = mix_out[c, me_b]

    def ia_copy(g, d):
        peer = (me_a + d) % n_aa
        return pltpu.make_async_remote_copy(
            src_ref=back.at[g, peer], dst_ref=field.at[g, 0, me_a],
            send_sem=ia_send.at[g, d], recv_sem=ia_recv.at[g, d],
            device_id=(peer, me_b), device_id_type=MESH,
        )

    def from_modes(c):
        for d in range(1, n_ba):
            ba_copy(1, c, d).wait_recv()
        for kk in range(kz_own):
            for q in range(0, q_part, 2):
                cols = []
                for qq in (q, q + 1):
                    cols.append(jnp.concatenate(
                        [mix_in[c, b, qq, kk].astype(F32) for b in range(n_ba)], axis=0
                    ).astype(BF))
                res = jnp.dot(x_inv_ref[...], jnp.concatenate(cols, axis=1), preferred_element_type=F32)
                for u in range(2):
                    for h in range(halves):
                        for a in range(n_aa):
                            first = (h * n_aa + a) * rows2
                            back[h * parts + c, a, kk, q + u] = res[
                                first : first + rows2, u * chans : (u + 1) * chans
                            ].astype(BF)

    def send_back(g):
        for d in range(1, n_aa):
            ia_copy(g, d).start()
        field[g, 0, me_a] = back[g, me_a]

    def ag_copy(t, g):
        n = 1 << (bits - 1 - t)
        return pltpu.make_async_remote_copy(
            src_ref=field.at[g, pl.ds(0, n)], dst_ref=field.at[g, pl.ds(n, n)],
            send_sem=ag_send.at[t, g], recv_sem=ag_recv.at[t, g],
            device_id=partner(t), device_id_type=MESH,
        )

    chunks = halves * parts
    steps = list(reversed(range(bits)))

    def gather_tick(tick):
        for n, t in enumerate(steps):
            g = tick - n
            if 0 <= g < chunks:
                if n == 0:
                    for d in range(1, n_aa):
                        ia_copy(g, d).wait_recv()
                else:
                    ag_copy(steps[n - 1], g).wait_recv()
                ag_copy(t, g).start()

    for tick in range(parts + 2):
        if tick < parts:
            to_modes(tick)
        if tick == 0:
            for p in range(2):
                for m in range(kx_own):
                    weight_fetch(p, m).wait()
        if 0 <= tick - 1 < parts:
            mix_modes(tick - 1)
        if 0 <= tick - 2 < parts:
            from_modes(tick - 2)
            send_back(tick - 2)
        if tick == parts + 1:
            for g in range(parts, chunks):
                send_back(g)
        if 0 <= tick - 4:
            gather_tick(tick - 4)
    ticks_done = max(parts + 2 - 4, 0)

    gap = kz + 8

    def spread(g):
        ag_copy(steps[-1], g).wait_recv()
        h, c = g // parts, g % parts

        def one(a, carry):
            for blk in range(n_ba):
                for kk in range(kz_own):
                    for q in range(q_part):
                        base = (((a * kz_own + kk) * n_ba + blk) * parts + c) * q_part + q
                        plane[h, pl.ds(base * rows2, rows2), :] = field[g, blk, a, kk, q].astype(F32)
            return carry

        lax.fori_loop(0, n_aa, one, 0)

    def flush(i):
        return pltpu.make_async_copy(
            xbuf.at[i % slots, :, pl.ds(0, 2 * kz)], out_ref.at[i], o_sem.at[i % slots]
        )

    def to_cells(i, carry):
        half = i // x_half
        local = i % x_half
        for k in range(0, kz, 2):
            cols = []
            for kk in (k, k + 1):
                first = kk * 2 * ky * x_half + local
                cols.append(jnp.concatenate(
                    [plane[half, pl.ds(first + 8 * g * x_half, 8, stride=x_half), :] for g in range(2 * ky // 8)],
                    axis=0,
                ).astype(BF))
            res = jnp.dot(y_inv_ref[me_b], jnp.concatenate(cols, axis=1), preferred_element_type=F32)
            for u in range(2):
                for g in range(2 * n_y // 8):
                    lines[0, pl.ds(8 * g * gap + k + u, 8, stride=gap), :] = res[
                        8 * g : 8 * g + 8, u * chans : (u + 1) * chans
                    ]

        @pl.when(i >= slots)
        def _():
            flush(i - slots).wait()

        for y in range(n_y):
            first = 2 * y * gap
            both = jnp.concatenate([lines[0, first : first + kz, :], lines[0, first + gap : first + gap + kz, :]], axis=0)
            xbuf[i % slots, y, 0 : 2 * kz, :] = both.astype(BF)
        flush(i).start()
        return carry

    cells_done = 0
    for tick in range(ticks_done, chunks + bits):
        gather_tick(tick)
        g = tick - bits
        if g >= 0:
            spread(g)
        ready = (g + 1) // parts * x_half
        upto = ready if tick == chunks + bits - 1 else min(ready, cells_done + 2)
        if upto > cells_done:
            lax.fori_loop(cells_done, upto, to_cells, 0)
            cells_done = upto
    for i in range(n_x - slots, n_x):
        flush(i).wait()

    for g in range(halves * parts):
        for s in range(bits):
            rs_copy(s, g).wait_send()
            ag_copy(s, g).wait_send()
        for d in range(1, n_aa):
            fa_copy(g, d).wait_send()
            ia_copy(g, d).wait_send()
    for which in range(2):
        for c in range(parts):
            for d in range(1, n_ba):
                ba_copy(which, c, d).wait_send()


def spectral(n_aa, n_ba, halves, parts, grid_features, weight_real, weight_imag, tables):
    n_x, n_y, depth, chans = grid_features.shape
    kx_own, ky, kz_own = weight_real.shape[:3]
    kz = kz_own * n_aa
    ky_own = ky // n_ba
    q_part = ky_own // parts
    bits = n_ba.bit_length() - 1
    rows2 = 2 * n_x // halves
    chunks = halves * parts
    slots = 4
    line_rows = max(2 * kz * (n_y + 8), 2 * n_y * (kz + 8))
    vm = pltpu.VMEM
    dma = pltpu.SemaphoreType.DMA

    def rs_shape(s):
        left = n_ba >> (s + 1)
        return vm((chunks, left, kz, q_part, rows2, chans), BF)

    outer = pl.BlockSpec(memory_space=pl.ANY)
    return pl.pallas_call(
        functools.partial(spectral_body, n_aa, n_ba, halves, parts, slots),
        in_specs=[outer] * 9,
        out_specs=outer,
        out_shape=jax.ShapeDtypeStruct((n_x, n_y, 2 * kz, chans), BF),
        scratch_shapes=[
            *[vm(t.shape, t.dtype) for t in tables],
            vm((kz_own, 2 * kx_own, chans), F32),
            vm((slots, n_y, depth, chans), BF),
            vm((2,) + weight_real.shape, BF),
            vm((2, line_rows, chans), F32),
            vm((halves, kz * 2 * ky * (n_x // halves), chans), F32),
            [rs_shape(t) for t in range(bits)], [rs_shape(t) for t in range(bits)],
            vm((chunks, n_aa, kz_own, q_part, rows2, chans), BF),
            vm((chunks, n_aa, kz_own, q_part, rows2, chans), BF),
            vm((parts, n_ba, kz_own, q_part, 2 * kx_own, chans), BF),
            vm((parts, n_ba, kz_own, q_part, 2 * kx_own, chans), BF),
            vm((parts, n_ba, q_part, kz_own, 2 * kx_own, chans), BF),
            vm((parts, n_ba, q_part, kz_own, 2 * kx_own, chans), BF),
            vm((chunks, n_aa, kz_own, q_part, rows2, chans), BF),
            vm((chunks, n_ba, n_aa, kz_own, q_part, rows2, chans), BF),
            dma((slots,)), dma((2, kx_own)),
            dma((bits, chunks)), dma((bits, chunks)),
            dma((chunks, n_aa)), dma((chunks, n_aa)),
            dma((2, parts, n_ba)), dma((2, parts, n_ba)),
            dma((chunks, n_aa)), dma((chunks, n_aa)),
            dma((bits, chunks)), dma((bits, chunks)), dma((slots,)), dma((len(tables),)),
        ],
        compiler_params=pltpu.CompilerParams(
            collective_id=0, has_side_effects=True, vmem_limit_bytes=67043328
        ),
    )(*tables, grid_features, weight_real, weight_imag)


def final_body(
    slots, table_in, w_in, bias_in, back_ref, x_ref, out_ref, table_ref, w_ref, bias_ref, xbuf, bbuf, obuf,
    w_half, bias_rows, in_sem, back_sem, out_sem, t_sem,
):
    n_x = x_ref.shape[0]
    n_y = x_ref.shape[1]
    c1 = 2.0 * math.sqrt(2.0 / math.pi)

    def fetch(i):
        return pltpu.make_async_copy(x_ref.at[i], xbuf.at[i % slots], in_sem.at[i % slots])

    def flush(i):
        return pltpu.make_async_copy(obuf.at[i % slots], out_ref.at[i], out_sem.at[i % slots])

    def fetch_back(i):
        return pltpu.make_async_copy(back_ref.at[i], bbuf.at[i % slots], back_sem.at[i % slots])

    small = ((table_in, table_ref), (w_in, w_ref), (bias_in, bias_ref))
    tables = [pltpu.make_async_copy(src, dst, t_sem.at[n]) for n, (src, dst) in enumerate(small)]
    for copy in tables:
        copy.start()
    for i in range(slots):
        fetch(i).start()
        fetch_back(i).start()
    for copy in tables:
        copy.wait()
    w_half[...] = (0.5 * w_ref[...].astype(F32)).astype(BF)
    bias_rows[...] = jnp.broadcast_to(bias_ref[...].astype(F32), bias_rows.shape).astype(BF)

    def step(i, carry):
        fetch(i).wait()
        fetch_back(i).wait()

        @pl.when(i >= slots)
        def _():
            flush(i - slots).wait()

        slot = i % slots
        for j in range(n_y):
            lhs = jnp.concatenate([xbuf[slot, j], table_ref[...]], axis=1)
            rhs = jnp.concatenate([w_half[...], bbuf[slot, j], bias_rows[...]], axis=0)
            half = jnp.dot(lhs, rhs, preferred_element_type=F32)
            inner = half * (c1 + (4.0 * c1 * 0.044715) * (half * half))
            obuf[slot, j] = (half + half * jnp.tanh(inner)).astype(BF)
        flush(i).start()

        @pl.when(i + slots < n_x)
        def _():
            fetch(i + slots).start()
            fetch_back(i + slots).start()

        return carry

    lax.fori_loop(0, n_x, step, 0)
    for i in range(n_x - slots, n_x):
        flush(i).wait()


def finish(grid_features, back, table, weight, bias):
    n_x, n_y, depth, chans = grid_features.shape
    modes = back.shape[2]
    extra = 16
    column = (np.arange(extra) == 0).astype(np.float32)
    table = np.concatenate([table.astype(np.float32), np.broadcast_to(column, (depth, extra))], axis=1)
    table = jnp.asarray((0.5 * table).astype(BF))
    slots = 3
    outer = pl.BlockSpec(memory_space=pl.ANY)
    return pl.pallas_call(
        functools.partial(final_body, slots),
        in_specs=[outer] * 5,
        out_specs=outer,
        out_shape=jax.ShapeDtypeStruct(grid_features.shape, BF),
        scratch_shapes=[
            pltpu.VMEM(table.shape, BF),
            pltpu.VMEM((chans, chans), BF),
            pltpu.VMEM((1, chans), BF),
            pltpu.VMEM((slots, n_y, depth, chans), BF),
            pltpu.VMEM((slots, n_y, modes, chans), BF),
            pltpu.VMEM((slots, n_y, depth, chans), BF),
            pltpu.VMEM((chans, chans), BF),
            pltpu.VMEM((extra, chans), BF),
            pltpu.SemaphoreType.DMA((slots,)),
            pltpu.SemaphoreType.DMA((slots,)),
            pltpu.SemaphoreType.DMA((slots,)),
            pltpu.SemaphoreType.DMA((3,)),
        ],
        compiler_params=pltpu.CompilerParams(vmem_limit_bytes=62 << 20),
        cost_estimate=pl.CostEstimate(
            flops=2 * n_x * n_y * depth * chans * (chans + modes),
            bytes_accessed=4 * n_x * n_y * depth * chans,
            transcendentals=n_x * n_y * depth * chans,
        ),
    )(table, weight, bias.reshape(1, chans), back, grid_features)


def per_device(
    n_aa, n_ba, grid_features, weight_real, weight_imag, mode_keep, local_weight, local_bias
):
    n_x, n_y, depth, chans = grid_features.shape
    kx_own, ky, kz_own = weight_real.shape[:3]
    nx, ny = n_x * n_aa, n_y * n_ba
    kx, kz, ky_own = kx_own * n_ba, kz_own * n_aa, ky // n_ba
    bits = n_ba.bit_length() - 1
    halves = max(n_x // 8, 1)
    parts = max(min(4, ky_own // 2), 1)
    x_half = n_x // halves

    c, s = phase_tables(depth, np.arange(depth), np.arange(kz))
    depth_fwd = np.concatenate([c, -s], axis=1).T.astype(BF)
    factor = np.where(np.arange(kz) == 0, 1.0, 2.0).astype(np.float32) / (nx * ny * depth)
    depth_inv = np.concatenate([c * factor, -s * factor], axis=1).astype(BF)

    y_fwd, y_inv = [], []
    order = np.arange(n_ba)
    block = np.zeros_like(order)
    for bit in range(bits):
        block = block + ((order >> (bits - 1 - bit)) & 1) * (1 << bit)
    for who in range(n_ba):
        ky_pos = ((block ^ who)[:, None] * ky_own + np.arange(ky_own)[None, :]).reshape(-1)
        ky_modes = kept_modes(ny, ky, ky_pos)
        own_y = who * n_y + np.arange(n_y)
        table = forward_table(ny, own_y, ky_modes)
        y_fwd.append(np.transpose(table, (3, 2, 0, 1)).reshape(2 * ky, 2 * n_y).astype(BF))
        table = inverse_table(ny, own_y, ky_modes)
        y_inv.append(np.transpose(table, (3, 2, 1, 0)).reshape(2 * n_y, 2 * ky).astype(BF))
    y_fwd, y_inv = np.stack(y_fwd), np.stack(y_inv)
    x_modes = kept_modes(nx, kx, np.arange(kx))
    x_fwd = forward_table(nx, np.arange(nx), x_modes)
    x_fwd = x_fwd.reshape(2, n_aa, halves, x_half, 2, n_ba, kx_own)
    x_fwd = np.transpose(x_fwd, (5, 4, 6, 2, 1, 0, 3)).reshape(2 * kx, 2 * nx).astype(BF)
    x_inv = inverse_table(nx, np.arange(nx), x_modes)
    x_inv = x_inv.reshape(2, n_ba, kx_own, 2, n_aa, halves, x_half)
    x_inv = np.transpose(x_inv, (5, 4, 3, 6, 1, 0, 2)).reshape(2 * nx, 2 * kx).astype(BF)
    back = spectral(
        n_aa, n_ba, halves, parts, grid_features, weight_real, weight_imag,
        (depth_fwd, y_fwd, y_inv, x_fwd, x_inv, mode_keep.T),
    )
    return finish(grid_features, back, depth_inv, local_weight, local_bias)


def solution(mesh):
    in_specs = (
        P("aa", "ba", None, None),
        P("ba", None, "aa", None, None),
        P("ba", None, "aa", None, None),
        P("ba", "aa"),
        P(),
        P(),
    )
    out_specs = P("aa", "ba", None, None)
    body = functools.partial(per_device, mesh.shape["aa"], mesh.shape["ba"])
    return jax.shard_map(body, mesh=mesh, in_specs=in_specs, out_specs=out_specs, check_vma=False)
```

time: 147 us -> 113 us (0.77)
  Pallas kernels: 125 us -> 112 us
  local copies, waits for them, and re-layouts: 9.9 us -> 0 us
  matrix products: 7.62 us -> 0 us
  other arithmetic: 4.18 us -> 0 us
    pallas_call x1, Pallas kernels: 101 us -> 86.1 us  [spectral(): pl.pallas_call(functools.partial(spectral_body, n_aa, n_ba, halves, parts...]
    dot_general x1 -> x0, matrix products: 7.62 us -> none  [per_device(): jnp.einsum('hsbakqpxc,pbsqry->hxyrakc', field, y_inv, preferred_element_t...]
    convert_element_type x1 -> x0, local copies, waits for them, and re-layouts: 6.53 us -> none  [per_device(): back = back.astype(BF).reshape(n_x, n_y, 2 * kz, chans)]
    convert_element_type x3 -> x0, other arithmetic: 3.35 us -> none  [the longest x2 1.97 us: finish(): bias = (bias.astype(F32)[None, :] * column[:, None]).astype(BF)]
    pallas_call x1, Pallas kernels: 24.3 us -> 26.1 us  [finish(): pl.pallas_call(functools.partial(final_body, slots), in_specs=[outer] * 5...]
where the time goes in v2:
time: 113 us; the launch traced here: 112 us
  Pallas kernels  112 us (99%)
    pallas_call x1, Pallas kernels, spectral(): pl.pallas_call(functools.partial(spectral_body, n_aa, n_ba, halves, parts...  86.1 us
    pallas_call x1, Pallas kernels, finish(): pl.pallas_call(functools.partial(final_body, slots), in_specs=[outer] * 5...  26.1 us

profile of v2, /device:TPU:27, one launch (start us, length us, event | category | flops | bytes accessed | tf_op | source)
XLA Modules:
  0.0 112.2 jit_solution(15156597938307449806)
XLA Ops:
  0.0 86.1 %shard_map.118.back_ref = bf16[16,32,32,128]{3,2,1,0:T(8,128)(2,1)} custom-call(bf16[32,256]{1,0:T(8,128)(2,1)} %constant.12.clone.depth_in, bf16[4,64,64]{2,1,0:T(8,128)(2,1)} %constant.13.clone.y_in, bf16[4,64,64]{2,1,0:T(8,128)(2,1)} %constant.14.clone.y_inv_in, bf16[64,256]{1,0:T(8,128)(2,1)} %constant.15.clone.x_fwd_in, ...), custom_call_target="tpu_custom_call" | custom-call | tf_op jit(solution)/shard_map/pallas_call | solution.py:446
  86.1 26.1 %shard_map.119 = bf16[16,32,256,128]{3,2,1,0:T(8,128)(2,1)} custom-call(bf16[256,48]{1,0:T(8,128)(2,1)} %constant.17.clone.table_in, bf16[128,128]{1,0:T(8,128)(2,1)} %w_in.1, bf16[1,128]{1,0:T(2,128)(2,1)} %bitcast.3, bf16[16,32,32,128]{3,2,1,0:T(8,128)(2,1)} %shard_map.118.back_ref, bf16[16,32,256,128]{3,2,1,0:T(8,128)(2,1)} %x_ref.3), custom_call_target="tpu_custom_call" | custom-call | flops 5368709120 | bytes 67108864 | tf_op jit(solution)/shard_map/pallas_call | solution.py:547
